TPU v7x, 256 devices: a whole 4x4x8 slice. The times are simulated.
256 devices in a mesh: freq: 32 (over z, x), rcv: 8 (over y, core).
Axes of the slice: x: 4, y: 4, z: 8, core: 2. Of those that a mesh axis runs over, the one named last changes fastest.
Arguments:
- primaries_start: float32 [512, 1024, 128], P(('rcv', 'freq')), may hold values from -6 to 6
- surface_operator: bfloat16 [512, 2, 384, 512], P('freq', None, 'rcv'), may hold values from -0.25 to 0.25
- data_spectra: bfloat16 [384, 512, 2, 128], P('rcv', 'freq'), may hold values from -6 to 6
- shrinkage: float32 [128], replicated, may hold values from 0.2 to 2
Outputs:
- primaries: float32 [512, 1024, 128], P(('rcv', 'freq'))
- residual_spectra: bfloat16 [384, 512, 2, 128], P('rcv', 'freq')
All inputs are finite; a program needn't handle non-finite values.
Results may differ from a plain program's by a relative error of at most 0.0085.
Values may be sent and summed in bfloat16 or wider, within the bound.
No kernel may reach another device: no remote copies, remote signals or barrier semaphores. Data moves between devices by JAX's collectives and lax.ppermute only.
A program may use at most 64 MiB of HBM per device.

v0:
```python
import math
import jax
import jax.numpy as jnp
from jax import lax
from jax.sharding import PartitionSpec as P

S = 128
NS = 512
T_SIZE = 1024
ITERS = 2
NF = 512


def transform_table(frequencies, samples):
    freq_index = jnp.arange(frequencies, dtype=jnp.int32)[:, None]
    sample_index = jnp.arange(samples, dtype=jnp.int32)[None, :]
    phase = freq_index * sample_index % samples
    angle = phase.astype(jnp.float32) * (2.0 * math.pi / samples)
    factor = math.sqrt(2.0 / samples)
    return jnp.stack([factor * jnp.cos(angle), -factor * jnp.sin(angle)], axis=1).astype(
        jnp.bfloat16
    )


def forward_product(block, piece):
    real_op = block[:, 0]
    imag_op = block[:, 1]
    real_in = piece[:, :, 0]
    imag_in = piece[:, :, 1]

    def product(left, right):
        return jnp.einsum("krn,nks->rks", left, right, preferred_element_type=jnp.float32)

    real_out = product(real_op, real_in) - product(imag_op, imag_in)
    imag_out = product(real_op, imag_in) + product(imag_op, real_in)
    return jnp.stack([real_out, imag_out], axis=2)


def adjoint_product(block, resid):
    real_op = block[:, 0]
    imag_op = block[:, 1]
    real_res = resid[:, :, 0]
    imag_res = resid[:, :, 1]

    def product(left, right):
        return jnp.einsum("krn,rks->nks", left, right, preferred_element_type=jnp.float32)

    real_dir = product(real_op, real_res) + product(imag_op, imag_res)
    imag_dir = product(real_op, imag_res) - product(imag_op, real_res)
    return jnp.stack([real_dir, imag_dir], axis=2)


def local(primaries_start, surface_operator, data_spectra, shrinkage):
    table = transform_table(NF, T_SIZE)
    primaries = primaries_start
    count_total = 2.0 * NF * NS * S
    residual = data_spectra
    for iteration in range(ITERS):
        local_spectra = jnp.einsum(
            "kct,nts->nkcs",
            table,
            primaries.astype(jnp.bfloat16),
            preferred_element_type=jnp.float32,
        ).astype(jnp.bfloat16)
        spectra = lax.all_to_all(local_spectra, "freq", split_axis=1, concat_axis=0, tiled=True)
        predicted = forward_product(
            surface_operator, lax.all_gather(spectra, "rcv", axis=0, tiled=True)
        )
        residual = (data_spectra.astype(jnp.float32) - predicted).astype(jnp.bfloat16)
        residual_sq = jnp.sum(jnp.square(residual.astype(jnp.float32)))
        direction = lax.psum_scatter(
            adjoint_product(surface_operator, residual), "rcv", scatter_dimension=0, tiled=True
        )
        direction_sq = jnp.sum(jnp.square(direction))
        residual_norm, direction_norm = lax.psum((residual_sq, direction_sq), ("freq", "rcv"))
        step_size = 0.5 * residual_norm / (direction_norm + 1e-06)
        threshold = shrinkage[None, None, :] * (step_size * jnp.sqrt(direction_norm / count_total))
        direction_low = direction.astype(jnp.bfloat16)
        update = jnp.einsum(
            "kct,nkcs->nts",
            table,
            lax.all_to_all(direction_low, "freq", split_axis=0, concat_axis=1, tiled=True),
            preferred_element_type=jnp.float32,
        )
        moved = primaries + step_size * update
        primaries = moved - jnp.clip(moved, -threshold, threshold)
    return (primaries, residual)


def solution(mesh):
    return jax.shard_map(
        local,
        mesh=mesh,
        in_specs=(
            P(("rcv", "freq"), None, None),
            P("freq", None, "rcv", None),
            P("rcv", "freq", None, None),
            P(),
        ),
        out_specs=(P(("rcv", "freq"), None, None), P("rcv", "freq", None, None)),
        check_vma=False,
    )
```

profile of v0, /device:TPU:1, one launch (start us, length us, event | category | flops | bytes accessed | tf_op | source)
XLA Modules:
  0.0 497.7 jit_solution(7442395549814731971)
XLA Ops:
  7.2 8.6 %multiply_convert_fusion = (bf16[512,1,1024]{2,0,1:T(8,128)(2,1)S(1)}, bf16[512,1,1024]{2,0,1:T(8,128)(2,1)S(1)}) fusion(), kind=kLoop, calls=%fused_computation.25 | loop fusion | flops 9437184 | bytes 2097152 | tf_op jit(solution)/shard_map/convert.1
  18.1 27.9 %all_to_all.72 = bf16[2,512,2,128]{3,0,2,1:T(2,128)(2,1)S(1)} all-to-all(bf16[2,512,2,128]{3,0,2,1:T(2,128)(2,1)S(1)} %copy.32), channel_id=1, replica_groups=mesh['freq'=32,'rcv'=8] {'freq'}, dimensions={1} | all-to-all | bytes 1048576 | tf_op jit(solution)/shard_map/all_to_all | solution.py:65
  47.5 33.2 %all-gather.3.cloned.1.call-done = bf16[512,16,2,128]{3,0,1,2:T(8,128)(2,1)} async-done(((bf16[64,16,2,128]{3,0,1,2:T(8,128)(2,1)}), bf16[512,16,2,128]{3,0,1,2:T(8,128)(2,1)}) %all-gather.3.cloned.1.call-update) | async-done | bytes 4194320 | tf_op jit(solution)/shard_map/all_gather | solution.py:67
  80.6 2.2 fusion.14
  82.8 2.0 fusion.15
  90.3 4.2 pad_maximum_fusion
  94.5 10.3 %copy.36 = f32[512,16,2,128]{3,1,2,0:T(8,128)} copy(f32[512,16,2,128]{0,3,1,2:T(8,128)} %pad_maximum_fusion) | data formatting | bytes 16777216 | tf_op jit(solution)/shard_map/stack | solution.py:50
  104.9 54.2 %reduce-scatter.3.cloned.1.call-done = f32[64,16,2,128]{3,1,2,0:T(8,128)} async-done(((f32[512,16,2,128]{3,1,2,0:T(8,128)}), f32[64,16,2,128]{3,1,2,0:T(8,128)}) %reduce-scatter.3.cloned.1.call-update) | async-done | bytes 1048592 | tf_op jit(solution)/shard_map/reduce_scatter | solution.py:71
  159.1 3.4 multiply_reduce_fusion.1
  162.4 9.5 %all-to-all-start.1 = ((bf16[64,16,2,128]{3,1,2,0:T(8,128)(2,1)}), bf16[64,16,2,128]{3,1,2,0:T(8,128)(2,1)S(1)}, u32[]{:S(2)}, u32[]{:S(2)}) async-start(bf16[64,16,2,128]{3,1,2,0:T(8,128)(2,1)} %get-tuple-element.23), calls=%async_computation.2 | async-start | bytes 1048576 | tf_op jit(solution)/shard_map/all_to_all | solution.py:82
  173.3 77.2 %all-reduce.1 = (f32[]{:T(128)}, f32[]{:T(128)}) all-reduce(f32[]{:T(128)} %get-tuple-element.18, f32[]{:T(128)} %get-tuple-element.22), channel_id=1, replica_groups=mesh['freq'=32,'rcv'=8] {'freq','rcv'}, use_global_device_ids=true, to_apply=%region_1.2 | all-reduce | flops 2 | bytes 16 | tf_op jit(solution)/shard_map/psum | solution.py:75
  252.7 2.8 minimum_subtract_fusion.1
  259.4 22.7 %all_to_all.73 = bf16[2,512,2,128]{3,2,0,1:T(2,128)(2,1)S(1)} all-to-all(bf16[2,512,2,128]{3,2,0,1:T(2,128)(2,1)S(1)} %copy.40), channel_id=1, replica_groups=mesh['freq'=32,'rcv'=8] {'freq'}, dimensions={1} | all-to-all | bytes 1048576 | tf_op jit(solution)/shard_map/all_to_all | solution.py:65
  283.5 30.9 %all-gather.5.cloned.1.call-done = bf16[512,16,2,128]{3,0,1,2:T(8,128)(2,1)} async-done(((bf16[64,16,2,128]{3,0,1,2:T(8,128)(2,1)}), bf16[512,16,2,128]{3,0,1,2:T(8,128)(2,1)}) %all-gather.5.cloned.1.call-update) | async-done | bytes 4194320 | tf_op jit(solution)/shard_map/all_gather | solution.py:67
  314.5 2.2 fusion.18
  316.7 2.0 fusion.19
  323.7 4.2 pad_maximum_fusion.1
  327.9 10.3 %copy.43 = f32[512,16,2,128]{3,1,2,0:T(8,128)} copy(f32[512,16,2,128]{0,3,1,2:T(8,128)} %pad_maximum_fusion.1) | data formatting | bytes 16777216 | tf_op jit(solution)/shard_map/stack | solution.py:50
  338.3 54.2 %reduce-scatter.5.cloned.1.call-done = f32[64,16,2,128]{3,1,2,0:T(8,128)} async-done(((f32[512,16,2,128]{3,1,2,0:T(8,128)}), f32[64,16,2,128]{3,1,2,0:T(8,128)}) %reduce-scatter.5.cloned.1.call-update) | async-done | bytes 1048592 | tf_op jit(solution)/shard_map/reduce_scatter | solution.py:71
  392.5 3.4 multiply_reduce_fusion
  395.8 9.5 %all-to-all-start.3 = ((bf16[64,16,2,128]{3,1,2,0:T(8,128)(2,1)}), bf16[64,16,2,128]{3,1,2,0:T(8,128)(2,1)S(1)}, u32[]{:S(2)}, u32[]{:S(2)}) async-start(bf16[64,16,2,128]{3,1,2,0:T(8,128)(2,1)} %get-tuple-element.21), calls=%async_computation.5 | async-start | bytes 1048576 | tf_op jit(solution)/shard_map/all_to_all | solution.py:82
  406.5 77.0 %all-reduce = (f32[]{:T(128)}, f32[]{:T(128)}) all-reduce(f32[]{:T(128)} %get-tuple-element.14, f32[]{:T(128)} %get-tuple-element.20), channel_id=1, replica_groups=mesh['freq'=32,'rcv'=8] {'freq','rcv'}, use_global_device_ids=true, to_apply=%region_6.7 | all-reduce | flops 2 | bytes 16 | tf_op jit(solution)/shard_map/psum | solution.py:75
  485.7 3.0 minimum_subtract_fusion
  488.6 2.5 copy.46
  (61 shorter events, 21.9 us)
Async XLA Ops:
  7.2 9.6 %copy-start.4 = (f32[2,1024,128]{2,1,0:T(8,128)S(1)}, f32[2,1024,128]{2,1,0:T(8,128)}, u32[]{:S(2)}) copy-start(f32[2,1024,128]{2,1,0:T(8,128)} %param.4) | copy-start | bytes 3145732
  7.2 73.5 %all-gather.3.cloned.1.call-start = ((), (), s32[]{:S(2)}) async-start(), calls=%async_computation.6 | async-start | bytes 4718592 | tf_op jit(solution)/shard_map/all_gather | solution.py:67
  15.8 1.0 copy-start.5
  15.8 1.7 copy-start.7
  17.5 63.1 %copy-start = (bf16[16,2,48,512]{3,2,1,0:T(8,128)(2,1)S(1)}, bf16[16,2,48,512]{3,2,1,0:T(8,128)(2,1)}, u32[]{:S(2)}) copy-start(bf16[16,2,48,512]{3,2,1,0:T(8,128)(2,1)} %param.5) | copy-start | bytes 4718596
  47.4 111.6 %reduce-scatter.3.cloned.1.call-start = ((), (), s32[]{:S(2)}) async-start(), calls=%async_computation.7 | async-start | bytes 9437184 | tf_op jit(solution)/shard_map/reduce_scatter | solution.py:71
  80.6 4.3 copy-start.1
  85.4 1.0 copy-start.3
  104.8 147.8 %copy-start.10 = (f32[128]{0:T(128)S(1)}, f32[128]{0:T(128)}, u32[]{:S(2)}) copy-start(f32[128]{0:T(128)} %param.7) | copy-start | bytes 1540
  162.4 90.2 %all-to-all-start.1 = ((bf16[64,16,2,128]{3,1,2,0:T(8,128)(2,1)}), bf16[64,16,2,128]{3,1,2,0:T(8,128)(2,1)S(1)}, u32[]{:S(2)}, u32[]{:S(2)}) async-start(bf16[64,16,2,128]{3,1,2,0:T(8,128)(2,1)} %get-tuple-element.23), calls=%async_computation.2 | async-start | bytes 1048576 | tf_op jit(solution)/shard_map/all_to_all | solution.py:82
  172.0 142.5 %all-gather.5.cloned.1.call-start = ((), (), s32[]{:S(2)}) async-start(), calls=%async_computation.8 | async-start | bytes 4718592 | tf_op jit(solution)/shard_map/all_gather | solution.py:67
  252.7 3.8 copy-start.6
  252.7 3.8 copy-start.8
  255.5 1.0 copy-start.11
  283.5 109.0 %reduce-scatter.5.cloned.1.call-start = ((), (), s32[]{:S(2)}) async-start(), calls=%async_computation.9 | async-start | bytes 9437184 | tf_op jit(solution)/shard_map/reduce_scatter | solution.py:71
  314.5 4.3 copy-start.2
  338.2 147.4 %copy-start.9 = (bf16[512,1,1024]{2,0,1:T(8,128)(2,1)S(1)}, bf16[512,1,1024]{2,0,1:T(8,128)(2,1)}, u32[]{:S(2)}) copy-start(bf16[512,1,1024]{2,0,1:T(8,128)(2,1)} %copy-done.7) | copy-start | bytes 3145732
  395.8 89.8 %all-to-all-start.3 = ((bf16[64,16,2,128]{3,1,2,0:T(8,128)(2,1)}), bf16[64,16,2,128]{3,1,2,0:T(8,128)(2,1)S(1)}, u32[]{:S(2)}, u32[]{:S(2)}) async-start(bf16[64,16,2,128]{3,1,2,0:T(8,128)(2,1)} %get-tuple-element.21), calls=%async_computation.5 | async-start | bytes 1048576 | tf_op jit(solution)/shard_map/all_to_all | solution.py:82
Sparse Core Ops, SparseCore 0:
  47.5 33.0 all-gather.2
  105.0 54.0 reduce-scatter.2
  283.6 30.8 all-gather.4
  338.4 54.0 reduce-scatter.4
where the time goes:
time: 499 us; the launch traced here: 498 us
  blocking collectives  205 us (41%)
  waiting for transfers between devices  173 us (35%)
  local copies, waits for them, and re-layouts  32.7 us (7%)
  other arithmetic  25.5 us (5%)
  matrix products  24.5 us (5%)
  starting transfers between devices  19.2 us (4%)
  between operations  18.3 us (4%)
    psum x2, blocking collectives, local(): lax.psum((residual_sq, direction_sq), ('freq', 'rcv'))  154 us
    reduce_scatter x2, waiting for transfers between devices, local(): lax.psum_scatter(adjoint_product(surface_operator, residual), 'rcv', scat...  108 us
    all_gather x2, waiting for transfers between devices, local(): lax.all_gather(spectra, 'rcv', axis=0, tiled=True)  64.1 us
    all_to_all x2, blocking collectives, local(): lax.all_to_all(local_spectra, 'freq', split_axis=1, concat_axis=0, tiled=...  50.6 us
    another operation x2, local copies, waits for them, and re-layouts, adjoint_product(): return jnp.stack([real_dir, imag_dir], axis=2)  20.6 us
    all_to_all x2, starting transfers between devices, local(): lax.all_to_all(direction_low, 'freq', split_axis=0, concat_axis=1, tiled=...  19.1 us
    dot_general x8, matrix products, product(): jnp.einsum('krn,nks->rks', left, right, preferred_element_type=jnp.float32)  10.5 us
  transfers between devices with their start and end apart: 6, of which 4 were waited for; matrix products, arithmetic and copies ran while one was open for 0% of the time, Pallas kernels for 0%

commit v1 on v0

--- a/solution.py
+++ b/solution.py
@@ -64,7 +64,10 @@
         ).astype(jnp.bfloat16)
         spectra = lax.all_to_all(local_spectra, "freq", split_axis=1, concat_axis=0, tiled=True)
         predicted = forward_product(
-            surface_operator, lax.all_gather(spectra, "rcv", axis=0, tiled=True)
+            surface_operator,
+            jnp.concatenate(
+                lax.all_to_all(jnp.stack([spectra] * lax.axis_size("rcv")), "rcv", 0, 0), axis=0
+            ),
         )
         residual = (data_spectra.astype(jnp.float32) - predicted).astype(jnp.bfloat16)
         residual_sq = jnp.sum(jnp.square(residual.astype(jnp.float32)))

time: 499 us -> 529 us (1.060)
  blocking collectives: 205 us -> 313 us
  waiting for transfers between devices: 173 us -> 98.5 us
  matrix products: 24.5 us -> 17.8 us
    all_to_all x0 -> x2, blocking collectives: none -> 109 us  [local(): lax.all_to_all(jnp.stack([spectra] * lax.axis_size('rcv')), 'rcv', 0, 0)]
    all_gather x2 -> x0, waiting for transfers between devices: 64.1 us -> none  [local(): lax.all_gather(spectra, 'rcv', axis=0, tiled=True)]
    reduce_scatter x2, waiting for transfers between devices: 108 us -> 98.5 us  [local(): lax.psum_scatter(adjoint_product(surface_operator, residual), 'rcv', scat...]
    dot_general x8, matrix products: 10.5 us -> 3.76 us  [product(): jnp.einsum('krn,nks->rks', left, right, preferred_element_type=jnp.float32)]
  transfers between devices with their start and end apart: 6 -> 4, of which waited for: 4 -> 2; matrix products, arithmetic and copies ran while one was open for 0% -> 0% of each run, Pallas kernels for 0% -> 0%
where the time goes in v1:
time: 529 us; the launch traced here: 528 us
  blocking collectives  313 us (59%)
  waiting for transfers between devices  98.5 us (19%)
  local copies, waits for them, and re-layouts  35.5 us (7%)
  other arithmetic  25.2 us (5%)
  starting transfers between devices  19.3 us (4%)
  between operations  18.2 us (3%)
  matrix products  17.8 us (3%)
    psum x2, blocking collectives, local(): lax.psum((residual_sq, direction_sq), ('freq', 'rcv'))  154 us
    all_to_all x2, blocking collectives, local(): lax.all_to_all(jnp.stack([spectra] * lax.axis_size('rcv')), 'rcv', 0, 0)  109 us
    reduce_scatter x2, waiting for transfers between devices, local(): lax.psum_scatter(adjoint_product(surface_operator, residual), 'rcv', scat...  98.5 us
    all_to_all x2, blocking collectives, local(): lax.all_to_all(local_spectra, 'freq', split_axis=1, concat_axis=0, tiled=...  50.3 us
    another operation x2, local copies, waits for them, and re-layouts, adjoint_product(): return jnp.stack([real_dir, imag_dir], axis=2)  20.6 us
    all_to_all x2, starting transfers between devices, local(): lax.all_to_all(direction_low, 'freq', split_axis=0, concat_axis=1, tiled=...  19.1 us
  transfers between devices with their start and end apart: 4, of which 2 were waited for; matrix products, arithmetic and copies ran while one was open for 0% of the time, Pallas kernels for 0%

profile of v1, /device:TPU:1, one launch (start us, length us, event | category | flops | bytes accessed | tf_op | source)
XLA Modules:
  0.0 528.1 jit_solution(3332944008992286740)
XLA Ops:
  7.2 8.6 %multiply_convert_fusion = (bf16[512,1,1024]{2,0,1:T(8,128)(2,1)S(1)}, bf16[512,1,1024]{2,0,1:T(8,128)(2,1)S(1)}) fusion(), kind=kLoop, calls=%fused_computation.25 | loop fusion | flops 9437184 | bytes 2097152 | tf_op jit(solution)/shard_map/convert.1
  18.1 27.9 %all_to_all.76 = bf16[2,512,2,128]{3,0,2,1:T(2,128)(2,1)S(1)} all-to-all(bf16[2,512,2,128]{3,0,2,1:T(2,128)(2,1)S(1)} %copy.52), channel_id=1, replica_groups=mesh['freq'=32,'rcv'=8] {'freq'}, dimensions={1} | all-to-all | bytes 1048576 | tf_op jit(solution)/shard_map/all_to_all | solution.py:65
  47.5 55.3 %all_to_all.77 = bf16[8,64,16,2,128]{4,1,2,3,0:T(8,128)(2,1)S(1)} all-to-all(bf16[8,64,16,2,128]{4,1,2,3,0:T(8,128)(2,1)S(1)} %stack.70), channel_id=1, replica_groups=mesh['freq'=32,'rcv'=8] {'rcv'}, dimensions={0} | all-to-all | bytes 8388608 | tf_op jit(solution)/shard_map/all_to_all | solution.py:69
  102.8 1.4 copy.56
  110.5 4.2 pad_maximum_fusion
  114.7 10.3 %copy.59 = f32[512,16,2,128]{3,1,2,0:T(8,128)} copy(f32[512,16,2,128]{0,3,1,2:T(8,128)} %pad_maximum_fusion) | data formatting | bytes 16777216 | tf_op jit(solution)/shard_map/stack | solution.py:50
  125.0 49.2 %reduce-scatter.3.cloned.1.call-done = f32[64,16,2,128]{3,1,2,0:T(8,128)} async-done(((f32[512,16,2,128]{3,1,2,0:T(8,128)}), f32[64,16,2,128]{3,1,2,0:T(8,128)}) %reduce-scatter.3.cloned.1.call-update) | async-done | bytes 1048592 | tf_op jit(solution)/shard_map/reduce_scatter | solution.py:74
  174.3 3.2 multiply_reduce_fusion.1
  177.5 9.5 %all-to-all-start.2 = ((bf16[64,16,2,128]{3,1,2,0:T(8,128)(2,1)}), bf16[64,16,2,128]{3,1,2,0:T(8,128)(2,1)S(1)}, u32[]{:S(2)}, u32[]{:S(2)}) async-start(bf16[64,16,2,128]{3,1,2,0:T(8,128)(2,1)} %get-tuple-element.25), calls=%async_computation.3 | async-start | bytes 1048576 | tf_op jit(solution)/shard_map/all_to_all | solution.py:85
  187.3 1.3 copy.62
  188.6 77.1 %all-reduce.1 = (f32[]{:T(128)}, f32[]{:T(128)}) all-reduce(f32[]{:T(128)} %get-tuple-element.20, f32[]{:T(128)} %get-tuple-element.24), channel_id=1, replica_groups=mesh['freq'=32,'rcv'=8] {'freq','rcv'}, use_global_device_ids=true, to_apply=%region_1.2 | all-reduce | flops 2 | bytes 16 | tf_op jit(solution)/shard_map/psum | solution.py:78
  267.8 2.8 minimum_subtract_fusion.1
  271.6 1.5 fusion.55
  274.4 22.4 %all_to_all.78 = bf16[2,512,2,128]{3,2,0,1:T(2,128)(2,1)S(1)} all-to-all(bf16[2,512,2,128]{3,2,0,1:T(2,128)(2,1)S(1)} %copy.63), channel_id=1, replica_groups=mesh['freq'=32,'rcv'=8] {'freq'}, dimensions={1} | all-to-all | bytes 1048576 | tf_op jit(solution)/shard_map/all_to_all | solution.py:65
  298.2 53.5 %all_to_all.79 = bf16[8,64,16,2,128]{4,1,2,3,0:T(8,128)(2,1)S(1)} all-to-all(bf16[8,64,16,2,128]{4,1,2,3,0:T(8,128)(2,1)S(1)} %stack.78), channel_id=1, replica_groups=mesh['freq'=32,'rcv'=8] {'rcv'}, dimensions={0} | all-to-all | bytes 8388608 | tf_op jit(solution)/shard_map/all_to_all | solution.py:69
  351.7 1.4 copy.67
  358.9 4.2 pad_maximum_fusion.1
  363.2 10.3 %copy.68 = f32[512,16,2,128]{3,1,2,0:T(8,128)} copy(f32[512,16,2,128]{0,3,1,2:T(8,128)} %pad_maximum_fusion.1) | data formatting | bytes 16777216 | tf_op jit(solution)/shard_map/stack | solution.py:50
  373.5 49.3 %reduce-scatter.5.cloned.1.call-done = f32[64,16,2,128]{3,1,2,0:T(8,128)} async-done(((f32[512,16,2,128]{3,1,2,0:T(8,128)}), f32[64,16,2,128]{3,1,2,0:T(8,128)}) %reduce-scatter.5.cloned.1.call-update) | async-done | bytes 1048592 | tf_op jit(solution)/shard_map/reduce_scatter | solution.py:74
  422.8 3.2 multiply_reduce_fusion
  426.0 9.5 %all-to-all-start.5 = ((bf16[64,16,2,128]{3,1,2,0:T(8,128)(2,1)}), bf16[64,16,2,128]{3,1,2,0:T(8,128)(2,1)S(1)}, u32[]{:S(2)}, u32[]{:S(2)}) async-start(bf16[64,16,2,128]{3,1,2,0:T(8,128)(2,1)} %get-tuple-element.23), calls=%async_computation.7 | async-start | bytes 1048576 | tf_op jit(solution)/shard_map/all_to_all | solution.py:85
  436.7 77.2 %all-reduce = (f32[]{:T(128)}, f32[]{:T(128)}) all-reduce(f32[]{:T(128)} %get-tuple-element.16, f32[]{:T(128)} %get-tuple-element.22), channel_id=1, replica_groups=mesh['freq'=32,'rcv'=8] {'freq','rcv'}, use_global_device_ids=true, to_apply=%region_6.7 | all-reduce | flops 2 | bytes 16 | tf_op jit(solution)/shard_map/psum | solution.py:78
  515.7 3.0 minimum_subtract_fusion
  518.7 2.5 copy.71
  (60 shorter events, 20.9 us)
Async XLA Ops:
  7.2 9.7 %copy-start.2 = (f32[2,1024,128]{2,1,0:T(8,128)S(1)}, f32[2,1024,128]{2,1,0:T(8,128)}, u32[]{:S(2)}) copy-start(f32[2,1024,128]{2,1,0:T(8,128)} %param.4) | copy-start | bytes 3145732
  7.2 167.1 %reduce-scatter.3.cloned.1.call-start = ((), (), s32[]{:S(2)}) async-start(), calls=%async_computation.8 | async-start | bytes 9437184 | tf_op jit(solution)/shard_map/reduce_scatter | solution.py:74
  15.8 1.0 copy-start.3
  15.8 1.7 copy-start.5
  102.8 1.4 copy-start
  105.6 1.0 copy-start.1
  125.0 142.7 %copy-start.8 = (f32[128]{0:T(128)S(1)}, f32[128]{0:T(128)}, u32[]{:S(2)}) copy-start(f32[128]{0:T(128)} %param.7) | copy-start | bytes 1540
  177.5 90.2 %all-to-all-start.2 = ((bf16[64,16,2,128]{3,1,2,0:T(8,128)(2,1)}), bf16[64,16,2,128]{3,1,2,0:T(8,128)(2,1)S(1)}, u32[]{:S(2)}, u32[]{:S(2)}) async-start(bf16[64,16,2,128]{3,1,2,0:T(8,128)(2,1)} %get-tuple-element.25), calls=%async_computation.3 | async-start | bytes 1048576 | tf_op jit(solution)/shard_map/all_to_all | solution.py:85
  187.1 235.7 %reduce-scatter.5.cloned.1.call-start = ((), (), s32[]{:S(2)}) async-start(), calls=%async_computation.9 | async-start | bytes 9437184 | tf_op jit(solution)/shard_map/reduce_scatter | solution.py:74
  267.8 3.8 copy-start.4
  267.8 3.8 copy-start.6
  270.6 1.0 copy-start.9
  373.5 142.2 %copy-start.7 = (bf16[512,1,1024]{2,0,1:T(8,128)(2,1)S(1)}, bf16[512,1,1024]{2,0,1:T(8,128)(2,1)}, u32[]{:S(2)}) copy-start(bf16[512,1,1024]{2,0,1:T(8,128)(2,1)} %copy-done.5) | copy-start | bytes 3145732
  426.0 89.7 %all-to-all-start.5 = ((bf16[64,16,2,128]{3,1,2,0:T(8,128)(2,1)}), bf16[64,16,2,128]{3,1,2,0:T(8,128)(2,1)S(1)}, u32[]{:S(2)}, u32[]{:S(2)}) async-start(bf16[64,16,2,128]{3,1,2,0:T(8,128)(2,1)} %get-tuple-element.23), calls=%async_computation.7 | async-start | bytes 1048576 | tf_op jit(solution)/shard_map/all_to_all | solution.py:85
Sparse Core Ops, SparseCore 0:
  125.2 49.0 reduce-scatter.2
  373.6 49.1 reduce-scatter.4
